TPU v7x, 512 devices: a whole 4x4x16 slice. The times are simulated.
512 devices in a mesh: space: 32 (over x, y, core), member: 16 (over z).
Axes of the slice: x: 4, y: 4, z: 16, core: 2. Of those that a mesh axis runs over, the one named last changes fastest.
Arguments:
- obs_pert: bfloat16 [80, 65536], P('member', 'space'), may hold values from -6 to 6
- innovation: bfloat16 [65536], P('space'), may hold values from -6 to 6
- obs_prec: bfloat16 [65536], P('space'), may hold values from 1 to 100
- obs_lists: int32 [6144, 256], P('space'), may hold values from 0 to 6143
- loc_weight: bfloat16 [6144, 256], P('space'), may hold values from 0.049804688 to 1
- send_rows: int32 [32, 16, 32], P('space'), may hold values from 0 to 11
- ocean_src: int32 [3072, 2], P('space'), may hold values from 0 to 511, as said below
- ocean_frac: float32 [3072], P('space'), may hold values from 0 to 1
- ocean_ens: bfloat16 [80, 3072, 2048], P(None, 'space', 'member'), may hold values from -6 to 6
Outputs:
- ocean_anal: bfloat16 [80, 3072, 2048], P(None, 'space', 'member')
Inputs may be any that keep to these rules, and one draw needn't show every extreme that they name: `ocean_src`: the two slots of one ocean block differ.
All inputs are finite; a program needn't handle non-finite values.
Results may differ from a plain program's by a relative error of at most 0.0064.
Values may be sent and summed in bfloat16 or wider, within the bound.
No kernel may reach another device: no remote copies, remote signals or barrier semaphores. Data moves between devices by JAX's collectives and lax.ppermute only.
A program may use at most 64 MiB of HBM per device.

v0:
```python
import jax
import jax.numpy as jnp
from jax import lax
from jax.sharding import PartitionSpec as P

ITERS = 12


def padded(cells, sides, width):
    for axis, dim in sides:
        count = lax.axis_size(axis)
        head = lax.slice_in_dim(cells, 0, width, axis=dim)
        tail = lax.slice_in_dim(cells, cells.shape[dim] - width, cells.shape[dim], axis=dim)
        cells = jnp.concatenate(
            [
                lax.ppermute(tail, axis, [(i, (i + 1) % count) for i in range(count)]),
                cells,
                lax.ppermute(head, axis, [((i + 1) % count, i) for i in range(count)]),
            ],
            axis=dim,
        )
    return cells


def copy_for_each(array, axis):
    devices = lax.axis_size(axis)
    return lax.all_to_all(
        jnp.broadcast_to(array[None], (devices, *array.shape)), axis, 0, 0, tiled=True
    )


def joined_along(pieces, dim):
    pieces = jnp.moveaxis(pieces, 0, dim)
    dims = pieces.shape
    return pieces.reshape(*dims[:dim], dims[dim] * dims[dim + 1], *dims[dim + 2 :])


def gather_directly(array, axis, dim):
    pieces = copy_for_each(array, axis)
    return joined_along(pieces, dim)


def transform(local_obs, loc_sel, innov_sel, prec_sel):
    members = local_obs.shape[0]
    obs_f32 = local_obs.astype(jnp.float32)
    obs_weight = loc_sel.astype(jnp.float32) * prec_sel.astype(jnp.float32)
    weighted = obs_f32 * obs_weight[None]
    gram = jnp.einsum("ibl,jbl->bij", weighted, obs_f32, precision=lax.Precision.HIGHEST)
    pulled = jnp.einsum(
        "ibl,bl->bi", weighted, innov_sel.astype(jnp.float32), precision=lax.Precision.HIGHEST
    )
    identity = jnp.eye(members, dtype=jnp.float32)
    precision_mat = (members - 1.0) * identity + gram
    scale_sum = jnp.trace(precision_mat, axis1=1, axis2=2)
    root_start = precision_mat / scale_sum[:, None, None]
    inverse_start = jnp.broadcast_to(identity, precision_mat.shape)

    def newton(iteration, carry):
        root_iter, inverse_iter = carry
        correction = 1.5 * identity - 0.5 * jnp.einsum(
            "bij,bjk->bik", inverse_iter, root_iter, precision=lax.Precision.HIGHEST
        )
        root_next = jnp.einsum(
            "bij,bjk->bik", root_iter, correction, precision=lax.Precision.HIGHEST
        )
        inverse_next = jnp.einsum(
            "bij,bjk->bik", correction, inverse_iter, precision=lax.Precision.HIGHEST
        )
        return (root_next, inverse_next)

    root_iter, inverse_iter = lax.fori_loop(0, ITERS, newton, (root_start, inverse_start))
    spread = jnp.sqrt((members - 1.0) / scale_sum)[:, None, None] * inverse_iter
    half_way = jnp.einsum("bij,bj->bi", inverse_iter, pulled, precision=lax.Precision.HIGHEST)
    mean_weight = (
        jnp.einsum("bij,bj->bi", inverse_iter, half_way, precision=lax.Precision.HIGHEST)
        / scale_sum[:, None]
    )
    return (spread + mean_weight[:, :, None]).astype(jnp.bfloat16)


def apply_weights(ensemble, mixed):
    ens_mean = jnp.mean(ensemble, axis=0, dtype=jnp.float32)
    deviation = (ensemble.astype(jnp.float32) - ens_mean[None]).astype(jnp.bfloat16)
    product = jnp.einsum("jol,oji->iol", deviation, mixed, preferred_element_type=jnp.float32)
    return (ens_mean[None] + product).astype(jnp.bfloat16)


def shards(
    obs_pert,
    innovation,
    obs_prec,
    obs_lists,
    loc_weight,
    send_rows,
    ocean_src,
    ocean_frac,
    ocean_ens,
):
    n_member = lax.axis_size("member")
    n_space = lax.axis_size("space")
    member_idx = lax.axis_index("member")
    tile_obs = obs_pert.shape[1]
    stacked = jnp.stack([innovation, obs_prec])
    pert_rim, info_rim = (
        padded(obs_pert, (("space", 1),), tile_obs),
        padded(stacked, (("space", 1),), tile_obs),
    )
    blocks = obs_lists.shape[0]
    group_len = blocks // n_member
    lists_mine = lax.dynamic_slice_in_dim(obs_lists, member_idx * group_len, group_len, 0)
    loc_mine = lax.dynamic_slice_in_dim(loc_weight, member_idx * group_len, group_len, 0)
    all_members = gather_directly(pert_rim, "member", 0)
    local_obs = all_members[:, lists_mine]
    innov_sel = info_rim[0][lists_mine]
    prec_sel = info_rim[1][lists_mine]
    weights = transform(local_obs, loc_mine, innov_sel, prec_sel)
    row_choice = lax.dynamic_index_in_dim(send_rows[0], member_idx, 0, keepdims=False)
    picked = weights[row_choice]
    arrived = lax.all_to_all(picked, "space", split_axis=0, concat_axis=0, tiled=True)
    mine_one = ocean_src[:, 0] // n_space == member_idx
    mine_two = ocean_src[:, 1] // n_space == member_idx
    coef_one = jnp.where(mine_one, 1.0 - ocean_frac, 0.0)[:, None, None]
    coef_two = jnp.where(mine_two, ocean_frac, 0.0)[:, None, None]
    take_one = arrived[ocean_src[:, 0] % n_space].astype(jnp.float32)
    take_two = arrived[ocean_src[:, 1] % n_space].astype(jnp.float32)
    partial_mix = coef_one * take_one + coef_two * take_two
    mixed = lax.psum(partial_mix, "member").astype(jnp.bfloat16)
    return apply_weights(ocean_ens, mixed)


def solution(mesh):
    return jax.shard_map(
        shards,
        mesh=mesh,
        in_specs=(
            P("member", "space"),
            P("space"),
            P("space"),
            P("space", None),
            P("space", None),
            P("space", None, None),
            P("space", None),
            P("space"),
            P(None, "space", "member"),
        ),
        out_specs=P(None, "space", "member"),
        check_vma=False,
    )
```

profile of v0, /device:TPU:6, one launch (start us, length us, event | category | flops | bytes accessed | tf_op | source)
XLA Modules:
  0.0 276.2 jit_solution(2189907386546934300)
XLA Ops:
  0.0 1.9 collective-permute-start
  1.9 5.8 %collective-permute-start.1 = (bf16[5,2048]{1,0:T(8,128)(2,1)}, bf16[5,2048]{1,0:T(8,128)(2,1)S(1)}, u32[]{:S(2)}, u32[]{:S(2)}) collective-permute-start(bf16[5,2048]{1,0:T(8,128)(2,1)} %param.11), channel_id=1, source_target_pairs={{16,0},{32,16},{48,32},{64,48},{80,64},{96,80},{112,96},{128,112},... | collective-permute-start | bytes 61448 | tf_op jit(solution)/shard_map/ppermute | solution.py:18
  7.7 1.9 collective-permute-done.1
  9.6 0.8 pad_maximum_fusion
  10.3 1.3 broadcast_in_dim.23
  11.7 15.4 %all-to-all-start = ((bf16[16,5,6144]{2,1,0:T(8,128)(2,1)}), bf16[16,5,6144]{2,1,0:T(8,128)(2,1)}, u32[]{:S(2)}, u32[]{:S(2)}) async-start(bf16[16,5,6144]{2,1,0:T(8,128)(2,1)} %broadcast_in_dim.23), calls=%async_computation | async-start | bytes 3145728 | tf_op jit(solution)/shard_map/all_to_all | solution.py:27
  27.1 1.9 collective-permute-start.2
  29.1 5.8 %collective-permute-start.3 = (bf16[2,2048]{1,0:T(2,128)(2,1)S(1)}, bf16[2,2048]{1,0:T(2,128)(2,1)S(1)}, u32[]{:S(2)}, u32[]{:S(2)}) collective-permute-start(bf16[2,2048]{1,0:T(2,128)(2,1)S(1)} %pad_maximum_fusion.2), channel_id=1, source_target_pairs={{16,0},{32,16},{48,32},{64,48},{80,64},{96,80},{112,96},{128,112},... | collective-permute-start | bytes 24584 | tf_op jit(solution)/shard_map/ppermute | solution.py:18
  34.8 0.8 compare_select_fusion
  35.6 0.7 fusion.25
  40.4 19.4 %gather_fusion.1 = bf16[3072]{0:T(1024)(128)(2,1)S(1)} fusion(bf16[6144]{0:T(1024)(128)(2,1)S(1)} %get-tuple-element.46, s32[3072]{0:T(1024)S(1)} %broadcast_clamp_fusion), kind=kCustom, calls=%fused_computation.1 | custom fusion | bytes 24576 | tf_op jit(solution)/shard_map/gather | solution.py:115
  59.7 19.4 %gather_fusion.2 = bf16[3072]{0:T(1024)(128)(2,1)S(1)} fusion(bf16[6144]{0:T(1024)(128)(2,1)S(1)} %get-tuple-element.45, s32[3072]{0:T(1024)S(1)} %broadcast_clamp_fusion), kind=kCustom, calls=%fused_computation.2 | custom fusion | bytes 24576 | tf_op jit(solution)/shard_map/gather | solution.py:114
  79.7 1.3 convert_multiply_fusion.3
  81.0 19.9 %all-to-all-done = bf16[16,5,6144]{2,1,0:T(8,128)(2,1)} async-done(((bf16[16,5,6144]{2,1,0:T(8,128)(2,1)}), bf16[16,5,6144]{2,1,0:T(8,128)(2,1)}, u32[]{:S(2)}, u32[]{:S(2)}) %all-to-all-start) | async-done | bytes 983072 | tf_op jit(solution)/shard_map/all_to_all | solution.py:27
  100.9 2.4 reshape.58
  103.3 1.8 copy.31
  105.1 11.5 %gather_fusion = bf16[3072,80]{1,0:T(8,128)(2,1)} fusion(bf16[80,6144]{0,1:T(8,128)(2,1)S(1)} %copy.31, s32[3072]{0:T(1024)S(1)} %broadcast_clamp_fusion), kind=kCustom, calls=%fused_computation | custom fusion | bytes 995328 | tf_op jit(solution)/shard_map/gather | solution.py:113
  116.6 1.4 copy.32
  118.1 1.5 select_reduce_fusion
  120.0 32.0 %while.13 = (s32[]{:T(128)}, f32[12,80,80]{1,2,0:T(8,128)S(1)}, f32[12,80,80]{2,1,0:T(8,128)S(1)}, s32[]{:T(128)}) while((s32[]{:T(128)}, f32[12,80,80]{1,2,0:T(8,128)S(1)}, f32[12,80,80]{2,1,0:T(8,128)S(1)}, s32[]{:T(128)}) %tuple.29), condition=%wide.region_3.4_spmd.clone, body=%wide.region_2.3_spmd.clone.sunk | while | flops 221350400 | bytes 4044853 | solution.py:71
  120.1 0.9 fusion.53
  121.0 0.6 fusion.54
  121.7 1.0 convolution_bitcast_fusion.2
  122.8 0.9 fusion.53
  123.7 0.6 fusion.54
  124.3 1.0 convolution_bitcast_fusion.2
  125.4 0.9 fusion.53
  127.0 1.0 convolution_bitcast_fusion.2
  128.1 0.9 fusion.53
  129.0 0.6 fusion.54
  129.7 1.0 convolution_bitcast_fusion.2
  130.8 0.9 fusion.53
  132.3 1.0 convolution_bitcast_fusion.2
  133.4 0.9 fusion.53
  135.0 1.0 convolution_bitcast_fusion.2
  136.1 0.9 fusion.53
  137.0 0.6 fusion.54
  137.7 1.0 convolution_bitcast_fusion.2
  138.8 0.9 fusion.53
  140.3 1.0 convolution_bitcast_fusion.2
  141.4 0.9 fusion.53
  143.0 1.0 convolution_bitcast_fusion.2
  144.1 0.9 fusion.53
  145.0 0.6 fusion.54
  145.6 1.0 convolution_bitcast_fusion.2
  146.7 0.9 fusion.53
  148.3 1.0 convolution_bitcast_fusion.2
  149.4 0.9 fusion.53
  151.0 1.0 convolution_bitcast_fusion.2
  152.6 0.9 fusion.18
  153.5 0.9 fusion.16
  154.7 1.5 gather_fusion.3
  156.2 6.2 %all-to-all-start.1 = ((bf16[32,80,80]{2,1,0:T(8,128)(2,1)}), bf16[32,80,80]{2,1,0:T(8,128)(2,1)S(1)}, u32[]{:S(2)}, u32[]{:S(2)}) async-start(bf16[32,80,80]{2,1,0:T(8,128)(2,1)} %gather_fusion.3), calls=%async_computation.1 | async-start | bytes 1310720 | tf_op jit(solution)/shard_map/all_to_all | solution.py:119
  162.5 1.7 fusion.4
  164.1 8.9 %all-to-all-done.1 = bf16[32,80,80]{2,1,0:T(8,128)(2,1)S(1)} async-done(((bf16[32,80,80]{2,1,0:T(8,128)(2,1)}), bf16[32,80,80]{2,1,0:T(8,128)(2,1)S(1)}, u32[]{:S(2)}, u32[]{:S(2)}) %all-to-all-start.1) | async-done | bytes 409632 | tf_op jit(solution)/shard_map/all_to_all | solution.py:119
  173.0 0.9 gather_fusion.4
  173.9 3.5 %copy.34 = bf16[96,80,80]{0,2,1:T(8,128)(2,1)} copy(bf16[96,80,80]{2,1,0:T(8,128)(2,1)S(1)} %gather_fusion.4) | data formatting | bytes 2457600 | tf_op jit(solution)/shard_map/gather | solution.py:124
  177.4 0.9 gather_fusion.5
  178.3 3.5 %copy.35 = bf16[96,80,80]{0,2,1:T(8,128)(2,1)} copy(bf16[96,80,80]{2,1,0:T(8,128)(2,1)S(1)} %gather_fusion.5) | data formatting | bytes 2457600 | tf_op jit(solution)/shard_map/gather | solution.py:125
  181.8 2.5 multiply_add_fusion
  184.2 81.5 %all-reduce.1 = bf16[96,80,80]{0,2,1:T(8,128)(2,1)} all-reduce(f32[96,80,80]{0,2,1:T(8,128)S(1)} %multiply_add_fusion), channel_id=1, replica_groups=mesh['space'=32,'member'=16] {'member'}, use_global_device_ids=true, to_apply=%region_4.5 | all-reduce | flops 614400 | bytes 3686400 | tf_op jit(solution)/shard_map/psum | solution.py:127
  265.8 5.9 %copy.36 = bf16[96,80,80]{1,2,0:T(8,128)(2,1)S(1)} copy(bf16[96,80,80]{0,2,1:T(8,128)(2,1)} %all-reduce.1) | data formatting | bytes 2457600 | tf_op jit(solution)/shard_map/convert_element_type | solution.py:127
  271.7 2.8 fusion.6
  274.4 1.8 copy.38
  (101 shorter events, 11.4 us)
Async XLA Ops:
  0.0 7.7 %collective-permute-start = (bf16[5,2048]{1,0:T(8,128)(2,1)}, bf16[5,2048]{1,0:T(8,128)(2,1)S(1)}, u32[]{:S(2)}, u32[]{:S(2)}) collective-permute-start(bf16[5,2048]{1,0:T(8,128)(2,1)} %param.11), channel_id=1, source_target_pairs={{0,16},{16,32},{32,48},{48,64},{64,80},{80,96},{96,112},{112,128},... | collective-permute-start | bytes 61448 | tf_op jit(solution)/shard_map/ppermute | solution.py:16
  1.9 7.7 %collective-permute-start.1 = (bf16[5,2048]{1,0:T(8,128)(2,1)}, bf16[5,2048]{1,0:T(8,128)(2,1)S(1)}, u32[]{:S(2)}, u32[]{:S(2)}) collective-permute-start(bf16[5,2048]{1,0:T(8,128)(2,1)} %param.11), channel_id=1, source_target_pairs={{16,0},{32,16},{48,32},{64,48},{80,64},{96,80},{112,96},{128,112},... | collective-permute-start | bytes 61448 | tf_op jit(solution)/shard_map/ppermute | solution.py:18
  11.6 15.4 %copy-start.6 = (bf16[2048]{0:T(1024)(128)(2,1)S(1)}, bf16[2048]{0:T(1024)(128)(2,1)}, u32[]{:S(2)}) copy-start(bf16[2048]{0:T(1024)(128)(2,1)} %param.13) | copy-start | bytes 12292
  11.6 15.4 %copy-start.7 = (bf16[2048]{0:T(1024)(128)(2,1)S(1)}, bf16[2048]{0:T(1024)(128)(2,1)}, u32[]{:S(2)}) copy-start(bf16[2048]{0:T(1024)(128)(2,1)} %param.12) | copy-start | bytes 12292
  11.6 26.5 %copy-start = (bf16[80,96,128]{2,1,0:T(8,128)(2,1)S(1)}, bf16[80,96,128]{2,1,0:T(8,128)(2,1)}, u32[]{:S(2)}) copy-start(bf16[80,96,128]{2,1,0:T(8,128)(2,1)} %param.19) | copy-start | bytes 5898244
  11.6 26.8 %copy-start.8 = (s32[96,2]{0,1:T(2,128)S(1)}, s32[96,2]{0,1:T(2,128)}, u32[]{:S(2)}) copy-start(s32[96,2]{0,1:T(2,128)} %param.17) | copy-start | bytes 2308
  11.7 27.4 %copy-start.13 = (f32[96]{0:T(128)S(1)}, f32[96]{0:T(128)}, u32[]{:S(2)}) copy-start(f32[96]{0:T(128)} %param.18) | copy-start | bytes 1156
  11.7 89.2 %all-to-all-start = ((bf16[16,5,6144]{2,1,0:T(8,128)(2,1)}), bf16[16,5,6144]{2,1,0:T(8,128)(2,1)}, u32[]{:S(2)}, u32[]{:S(2)}) async-start(bf16[16,5,6144]{2,1,0:T(8,128)(2,1)} %broadcast_in_dim.23), calls=%async_computation | async-start | bytes 3145728 | tf_op jit(solution)/shard_map/all_to_all | solution.py:27
  27.1 13.0 %collective-permute-start.2 = (bf16[2,2048]{1,0:T(2,128)(2,1)S(1)}, bf16[2,2048]{1,0:T(2,128)(2,1)S(1)}, u32[]{:S(2)}, u32[]{:S(2)}) collective-permute-start(bf16[2,2048]{1,0:T(2,128)(2,1)S(1)} %pad_maximum_fusion.2), channel_id=1, source_target_pairs={{0,16},{16,32},{32,48},{48,64},{64,80},{80,96},{96,112},{112,128},... | collective-permute-start | bytes 24584 | tf_op jit(solution)/shard_map/ppermute | solution.py:16
  29.1 11.1 %collective-permute-start.3 = (bf16[2,2048]{1,0:T(2,128)(2,1)S(1)}, bf16[2,2048]{1,0:T(2,128)(2,1)S(1)}, u32[]{:S(2)}, u32[]{:S(2)}) collective-permute-start(bf16[2,2048]{1,0:T(2,128)(2,1)S(1)} %pad_maximum_fusion.2), channel_id=1, source_target_pairs={{16,0},{32,16},{48,32},{64,48},{80,64},{96,80},{112,96},{128,112},... | collective-permute-start | bytes 24584 | tf_op jit(solution)/shard_map/ppermute | solution.py:18
  118.0 1.9 copy-start.3
  120.0 32.0 %copy-start.4 = (f32[12,256]{1,0:T(8,128)S(1)}, f32[12,256]{1,0:T(8,128)}, u32[]{:S(2)}) copy-start(f32[12,256]{1,0:T(8,128)} %convert_multiply_fusion.3) | copy-start | bytes 36868
  120.0 32.0 %copy-start.5 = (bf16[12,256,1]{1,2,0:T(2,128)(2,1)S(1)}, bf16[12,256,1]{1,2,0:T(2,128)(2,1)}, u32[]{:S(2)}) copy-start(bf16[12,256,1]{1,2,0:T(2,128)(2,1)} %reshape.121) | copy-start | bytes 18436
  153.5 8.9 %copy-start.11 = (s32[96]{0:T(128)S(1)}, s32[96]{0:T(128)}, u32[]{:S(2)}) copy-start(s32[96]{0:T(128)} %get-tuple-element.55) | copy-start | bytes 1156
  153.5 8.9 %copy-start.12 = (s32[96]{0:T(128)S(1)}, s32[96]{0:T(128)}, u32[]{:S(2)}) copy-start(s32[96]{0:T(128)} %get-tuple-element.56) | copy-start | bytes 1156
  153.5 9.0 %copy-start.1 = (f32[96,128]{1,0:T(8,128)S(1)}, f32[96,128]{1,0:T(8,128)}, u32[]{:S(2)}) copy-start(f32[96,128]{1,0:T(8,128)} %broadcast_multiply_fusion) | copy-start | bytes 147460
  156.2 16.8 %all-to-all-start.1 = ((bf16[32,80,80]{2,1,0:T(8,128)(2,1)}), bf16[32,80,80]{2,1,0:T(8,128)(2,1)S(1)}, u32[]{:S(2)}, u32[]{:S(2)}) async-start(bf16[32,80,80]{2,1,0:T(8,128)(2,1)} %gather_fusion.3), calls=%async_computation.1 | async-start | bytes 1310720 | tf_op jit(solution)/shard_map/all_to_all | solution.py:119
  178.3 3.5 %copy-start.9 = (f32[96]{0:T(128)S(1)}, f32[96]{0:T(128)}, u32[]{:S(2)}) copy-start(f32[96]{0:T(128)} %get-tuple-element.53) | copy-start | bytes 1156
  178.3 3.5 %copy-start.10 = (f32[96]{0:T(128)S(1)}, f32[96]{0:T(128)}, u32[]{:S(2)}) copy-start(f32[96]{0:T(128)} %get-tuple-element.54) | copy-start | bytes 1156
  265.8 5.9 %copy-start.2 = (f32[96,128]{1,0:T(8,128)S(1)}, f32[96,128]{1,0:T(8,128)}, u32[]{:S(2)}) copy-start(f32[96,128]{1,0:T(8,128)} %broadcast_multiply_fusion) | copy-start | bytes 147460
where the time goes:
time: 277 us; the launch traced here: 276 us
  blocking collectives  81.5 us (29%)
  local copies, waits for them, and re-layouts  76.9 us (28%)
  matrix products  37 us (13%)
  starting transfers between devices  36.9 us (13%)
  waiting for transfers between devices  30.6 us (11%)
  other arithmetic  12.1 us (4%)
    psum x1, blocking collectives, shards(): mixed = lax.psum(partial_mix, 'member').astype(jnp.bfloat16)  81.5 us
    gather x2, local copies, waits for them, and re-layouts, shards(): innov_sel = info_rim[0][lists_mine]  20 us
    all_to_all x1, waiting for transfers between devices, copy_for_each(): lax.all_to_all(jnp.broadcast_to(array[None], (devices, *array.shape)), ax...  19.9 us
    gather x1, local copies, waits for them, and re-layouts, shards(): prec_sel = info_rim[1][lists_mine]  19.4 us
    all_to_all x1, starting transfers between devices, copy_for_each(): lax.all_to_all(jnp.broadcast_to(array[None], (devices, *array.shape)), ax...  15.4 us
    gather x2, local copies, waits for them, and re-layouts, shards(): local_obs = all_members[:, lists_mine]  12.9 us
    dot_general x12, matrix products, newton(): jnp.einsum('bij,bjk->bik', root_iter, correction, precision=lax.Precision...  11.7 us
    ppermute x2, starting transfers between devices, padded(): lax.ppermute(head, axis, [((i + 1) % count, i) for i in range(count)])  11.5 us
  transfers between devices with their start and end apart: 6, of which 3 were waited for; matrix products, arithmetic and copies ran while one was open for 17% of the time, Pallas kernels for 0%

commit v1 on v0

--- a/solution.py
+++ b/solution.py
@@ -124,7 +124,7 @@
     take_one = arrived[ocean_src[:, 0] % n_space].astype(jnp.float32)
     take_two = arrived[ocean_src[:, 1] % n_space].astype(jnp.float32)
     partial_mix = coef_one * take_one + coef_two * take_two
-    mixed = lax.psum(partial_mix, "member").astype(jnp.bfloat16)
+    mixed = jnp.sum(lax.all_gather(partial_mix, "member"), axis=0).astype(jnp.bfloat16)
     return apply_weights(ocean_ens, mixed)
 
 

time: 277 us -> 769 us (2.78)
  waiting for transfers between devices: 30.6 us -> 577 us
  blocking collectives: 81.5 us -> 0 us
  other arithmetic: 12.1 us -> 31.3 us
  between operations: 0.37 us -> 13.7 us
    all_gather x0 -> x1, waiting for transfers between devices: none -> 540 us  [shards(): lax.all_gather(partial_mix, 'member')]
    psum x1 -> x0, blocking collectives: 81.5 us -> none  [shards(): mixed = lax.psum(partial_mix, 'member').astype(jnp.bfloat16)]
    reduce_sum x0 -> x1, other arithmetic: none -> 21.6 us  [shards(): jnp.sum(lax.all_gather(partial_mix, 'member'), axis=0).astype(jnp.bfloat16)]
  transfers between devices with their start and end apart: 6 -> 7, of which waited for: 3 -> 4; matrix products, arithmetic and copies ran while one was open for 17% -> 6% of each run, Pallas kernels for 0% -> 0%
where the time goes in v1:
time: 769 us; the launch traced here: 767 us
  waiting for transfers between devices  577 us (75%)
  local copies, waits for them, and re-layouts  71.2 us (9%)
  starting transfers between devices  37.1 us (5%)
  matrix products  36.2 us (5%)
  other arithmetic  31.3 us (4%)
  between operations  13.7 us (2%)
    all_gather x1, waiting for transfers between devices, shards(): lax.all_gather(partial_mix, 'member')  540 us
    all_to_all x1, waiting for transfers between devices, copy_for_each(): lax.all_to_all(jnp.broadcast_to(array[None], (devices, *array.shape)), ax...  24.8 us
    reduce_sum x1, other arithmetic, shards(): jnp.sum(lax.all_gather(partial_mix, 'member'), axis=0).astype(jnp.bfloat16)  21.6 us
    gather x2, local copies, waits for them, and re-layouts, shards(): innov_sel = info_rim[0][lists_mine]  19.4 us
    gather x1, local copies, waits for them, and re-layouts, shards(): prec_sel = info_rim[1][lists_mine]  19.4 us
  transfers between devices with their start and end apart: 7, of which 4 were waited for; matrix products, arithmetic and copies ran while one was open for 6% of the time, Pallas kernels for 0%

profile of v1, /device:TPU:6, one launch (start us, length us, event | category | flops | bytes accessed | tf_op | source)
XLA Modules:
  0.0 767.3 jit_solution(15818956337043159522)
XLA Ops:
  6.5 1.9 collective-permute-start
  8.5 5.8 collective-permute-start.1
  14.2 1.9 collective-permute-done.1
  16.1 0.8 pad_maximum_fusion
  16.9 1.3 broadcast_in_dim.23
  18.2 15.3 %all-to-all-start = ((bf16[16,5,6144]{2,1,0:T(8,128)(2,1)}), bf16[16,5,6144]{2,1,0:T(8,128)(2,1)S(1)}, u32[]{:S(2)}, u32[]{:S(2)}) async-start(bf16[16,5,6144]{2,1,0:T(8,128)(2,1)} %broadcast_in_dim.23), calls=%async_computation | async-start | bytes 3145728 | tf_op jit(solution)/shard_map/all_to_all | solution.py:27
  33.6 1.9 collective-permute-start.2
  35.5 5.8 collective-permute-start.3
  41.3 0.8 compare_select_fusion
  42.0 0.7 fusion.26
  43.0 19.4 %gather_fusion.1 = bf16[3072]{0:T(1024)(128)(2,1)S(1)} fusion(bf16[6144]{0:T(1024)(128)(2,1)S(1)} %get-tuple-element.52, s32[3072]{0:T(1024)S(1)} %broadcast_clamp_fusion), kind=kCustom, calls=%fused_computation.1 | custom fusion | bytes 24576 | tf_op jit(solution)/shard_map/gather | solution.py:115
  62.4 19.4 %gather_fusion.2 = bf16[3072]{0:T(1024)(128)(2,1)S(1)} fusion(bf16[6144]{0:T(1024)(128)(2,1)S(1)} %get-tuple-element.51, s32[3072]{0:T(1024)S(1)} %broadcast_clamp_fusion), kind=kCustom, calls=%fused_computation.2 | custom fusion | bytes 24576 | tf_op jit(solution)/shard_map/gather | solution.py:114
  81.8 0.7 convert_multiply_fusion.5
  82.5 24.8 %all-to-all-done = bf16[16,5,6144]{2,1,0:T(8,128)(2,1)S(1)} async-done(((bf16[16,5,6144]{2,1,0:T(8,128)(2,1)}), bf16[16,5,6144]{2,1,0:T(8,128)(2,1)S(1)}, u32[]{:S(2)}, u32[]{:S(2)}) %all-to-all-start) | async-done | bytes 983072 | tf_op jit(solution)/shard_map/all_to_all | solution.py:27
  107.8 0.9 copy.50
  108.7 9.2 %gather_fusion = bf16[3072,80]{1,0:T(8,128)(2,1)S(1)} fusion(bf16[80,6144]{0,1:T(8,128)(2,1)S(1)} %copy.50, s32[3072]{0:T(1024)S(1)} %broadcast_clamp_fusion), kind=kCustom, calls=%fused_computation | custom fusion | bytes 995328 | tf_op jit(solution)/shard_map/gather | solution.py:113
  118.1 0.7 select_reduce_fusion
  119.2 32.0 %while.13 = (s32[]{:T(128)}, f32[12,80,80]{1,2,0:T(8,128)S(1)}, f32[12,80,80]{2,1,0:T(8,128)S(1)}, s32[]{:T(128)}) while((s32[]{:T(128)}, f32[12,80,80]{1,2,0:T(8,128)S(1)}, f32[12,80,80]{2,1,0:T(8,128)S(1)}, s32[]{:T(128)}) %tuple.31), condition=%wide.region_3.4_spmd.clone, body=%wide.region_2.3_spmd.clone.sunk | while | flops 221350400 | bytes 4044853 | solution.py:71
  119.3 0.9 fusion.54
  120.2 0.6 fusion.55
  120.9 1.0 convolution_bitcast_fusion.2
  122.0 0.9 fusion.54
  122.9 0.6 fusion.55
  123.5 1.0 convolution_bitcast_fusion.2
  124.6 0.9 fusion.54
  125.6 0.6 fusion.55
  126.2 1.0 convolution_bitcast_fusion.2
  127.3 0.9 fusion.54
  128.2 0.6 fusion.55
  128.9 1.0 convolution_bitcast_fusion.2
  130.0 0.9 fusion.54
  131.5 1.0 convolution_bitcast_fusion.2
  132.6 0.9 fusion.54
  134.2 1.0 convolution_bitcast_fusion.2
  135.3 0.9 fusion.54
  136.2 0.6 fusion.55
  136.9 1.0 convolution_bitcast_fusion.2
  138.0 0.9 fusion.54
  139.5 1.0 convolution_bitcast_fusion.2
  140.6 0.9 fusion.54
  142.2 1.0 convolution_bitcast_fusion.2
  143.3 0.9 fusion.54
  144.2 0.6 fusion.55
  144.9 1.0 convolution_bitcast_fusion.2
  146.0 0.9 fusion.54
  147.5 1.0 convolution_bitcast_fusion.2
  148.6 0.9 fusion.54
  150.2 1.0 convolution_bitcast_fusion.2
  151.8 0.9 fusion.19
  152.7 0.9 fusion.17
  153.9 1.5 gather_fusion.3
  155.3 6.2 all-to-all-start.1
  161.9 10.3 %all-to-all-done.1 = bf16[32,80,80]{2,1,0:T(8,128)(2,1)S(1)} async-done(((bf16[32,80,80]{2,1,0:T(8,128)(2,1)}), bf16[32,80,80]{2,1,0:T(8,128)(2,1)S(1)}, u32[]{:S(2)}, u32[]{:S(2)}) %all-to-all-start.1) | async-done | bytes 409632 | tf_op jit(solution)/shard_map/all_to_all | solution.py:119
  172.1 0.9 gather_fusion.4
  173.1 2.1 gather_fusion.5
  175.2 4.1 fusion.5
  179.3 5.6 copy.53
  184.9 1.5 copy-done
  186.7 1.7 fusion.4
  188.4 540.1 %all-gather.2.cloned.1.call-done = f32[16,96,80,80]{1,3,2,0:T(8,128)} async-done(((f32[1,96,80,80]{1,3,2,0:T(8,128)}), f32[16,96,80,80]{1,3,2,0:T(8,128)}) %all-gather.2.cloned.1.call-update) | async-done | bytes 39321616 | tf_op jit(solution)/shard_map/all_gather | solution.py:127
  728.5 21.6 %reduce_sum.30 = bf16[96,80,80]{0,2,1:T(8,128)(2,1)} reduce(f32[16,96,80,80]{1,3,2,0:T(8,128)} %all-gather.2.cloned.1.call-done, f32[]{:T(128)} %constant.70.clone.1), dimensions={0}, to_apply=%region_4.5 | reduce | flops 9216000 | bytes 40550404 | tf_op jit(solution)/shard_map/reduce_sum | solution.py:127
  750.1 5.9 copy.56
  755.9 2.8 fusion.7
  758.7 1.8 copy.58
  (85 shorter events, 7.6 us)
Async XLA Ops:
  6.5 7.7 %collective-permute-start = (bf16[5,2048]{1,0:T(8,128)(2,1)}, bf16[5,2048]{1,0:T(8,128)(2,1)S(1)}, u32[]{:S(2)}, u32[]{:S(2)}) collective-permute-start(bf16[5,2048]{1,0:T(8,128)(2,1)} %param.11), channel_id=1, source_target_pairs={{0,16},{16,32},{32,48},{48,64},{64,80},{80,96},{96,112},{112,128},... | collective-permute-start | bytes 61448 | tf_op jit(solution)/shard_map/ppermute | solution.py:16
  8.5 7.7 collective-permute-start.1
  18.2 15.3 %copy-start.1 = (bf16[2048]{0:T(1024)(128)(2,1)S(1)}, bf16[2048]{0:T(1024)(128)(2,1)}, u32[]{:S(2)}) copy-start(bf16[2048]{0:T(1024)(128)(2,1)} %param.13) | copy-start | bytes 12292
  18.2 15.4 %copy-start.2 = (bf16[2048]{0:T(1024)(128)(2,1)S(1)}, bf16[2048]{0:T(1024)(128)(2,1)}, u32[]{:S(2)}) copy-start(bf16[2048]{0:T(1024)(128)(2,1)} %param.12) | copy-start | bytes 12292
  18.2 89.1 %all-to-all-start = ((bf16[16,5,6144]{2,1,0:T(8,128)(2,1)}), bf16[16,5,6144]{2,1,0:T(8,128)(2,1)S(1)}, u32[]{:S(2)}, u32[]{:S(2)}) async-start(bf16[16,5,6144]{2,1,0:T(8,128)(2,1)} %broadcast_in_dim.23), calls=%async_computation | async-start | bytes 3145728 | tf_op jit(solution)/shard_map/all_to_all | solution.py:27
  33.6 9.2 %collective-permute-start.2 = (bf16[2,2048]{1,0:T(2,128)(2,1)S(1)}, bf16[2,2048]{1,0:T(2,128)(2,1)S(1)}, u32[]{:S(2)}, u32[]{:S(2)}) collective-permute-start(bf16[2,2048]{1,0:T(2,128)(2,1)S(1)} %pad_maximum_fusion.2), channel_id=1, source_target_pairs={{0,16},{16,32},{32,48},{48,64},{64,80},{80,96},{96,112},{112,128},... | collective-permute-start | bytes 24584 | tf_op jit(solution)/shard_map/ppermute | solution.py:16
  35.5 7.3 collective-permute-start.3
  152.7 9.1 %copy-start.3 = (s32[96,2]{0,1:T(2,128)S(1)}, s32[96,2]{0,1:T(2,128)}, u32[]{:S(2)}) copy-start(s32[96,2]{0,1:T(2,128)} %param.17) | copy-start | bytes 2308
  152.7 9.2 %copy-start.4 = (f32[96]{0:T(128)S(1)}, f32[96]{0:T(128)}, u32[]{:S(2)}) copy-start(f32[96]{0:T(128)} %param.18) | copy-start | bytes 1156
  155.3 16.8 %all-to-all-start.1 = ((bf16[32,80,80]{2,1,0:T(8,128)(2,1)}), bf16[32,80,80]{2,1,0:T(8,128)(2,1)S(1)}, u32[]{:S(2)}, u32[]{:S(2)}) async-start(bf16[32,80,80]{2,1,0:T(8,128)(2,1)} %gather_fusion.3), calls=%async_computation.1 | async-start | bytes 1310720 | tf_op jit(solution)/shard_map/all_to_all | solution.py:119
  161.6 566.9 %all-gather.2.cloned.1.call-start = ((), (), s32[]{:S(2)}) async-start(), calls=%async_computation.2 | async-start | bytes 55705600 | tf_op jit(solution)/shard_map/all_gather | solution.py:127
  184.9 1.5 copy-start
Sparse Core Ops, SparseCore 0:
  185.0 543.4 all-gather.1
